TPU v7x, 32 devices: a whole 2x2x4 slice. The times are simulated.
32 devices in a mesh: owner: 4 (over y, core), rows: 8 (over z, x).
Axes of the slice: x: 2, y: 2, z: 4, core: 2. Of those that a mesh axis runs over, the one named last changes fastest.
Arguments:
- train_gate: float32 [128, 2048, 768], P('owner', 'rows'), may hold values from -0.125 to 0.125
- train_up: float32 [128, 2048, 768], P('owner', 'rows'), may hold values from -0.125 to 0.125
- router_weight: float32 [2048, 128], P('rows', 'owner'), may hold values from -0.125 to 0.125
- router_gain: float32 [2048], P('rows'), may hold values from 0.25 to 1.75
Outputs:
- ready_gate: bfloat16 [128, 768, 2048], P(('owner', 'rows'))
- ready_up: bfloat16 [128, 768, 2048], P(('owner', 'rows'))
- serve_router: bfloat16 [2048, 128], replicated
All inputs are finite; a program needn't handle non-finite values.
Results may differ from a plain program's by a relative error of at most 0.001.
Values may be sent and summed in bfloat16 or wider, within the bound.
A program may use at most 192 MiB of HBM per device.

v0:
```python
import jax
import jax.numpy as jnp
from jax import lax
from jax.sharding import PartitionSpec as P


def on_device(train_gate, train_up, router_weight, router_gain):
    narrow_gate, narrow_up = (train_gate.astype(jnp.bfloat16), train_up.astype(jnp.bfloat16))
    ready_gate, ready_up = (
        lax.all_to_all(narrow_gate, "rows", split_axis=0, concat_axis=1, tiled=True),
        lax.all_to_all(narrow_up, "rows", split_axis=0, concat_axis=1, tiled=True),
    )
    ready_gate = jnp.transpose(ready_gate, (0, 2, 1))
    ready_up = jnp.transpose(ready_up, (0, 2, 1))
    part_router = (router_weight * router_gain[:, None]).astype(jnp.bfloat16)
    row_router = lax.all_gather(part_router, "rows", axis=0, tiled=True)
    serve_router = lax.all_gather(row_router, "owner", axis=1, tiled=True)
    return (ready_gate, ready_up, serve_router)


def solution(mesh):
    placed = (P("owner", "rows", None), P("owner", "rows", None), P("rows", "owner"), P("rows"))
    return jax.shard_map(
        on_device,
        mesh=mesh,
        in_specs=placed,
        out_specs=(P(("owner", "rows"), None, None), P(("owner", "rows"), None, None), P()),
        check_vma=False,
    )
```

profile of v0, /device:TPU:0, one launch (start us, length us, event | category | flops | bytes accessed | tf_op | source)
XLA Modules:
  0.0 672.7 jit_solution(13268045616997217038)
XLA Ops:
  0.6 13.2 %convert_element_type.9 = bf16[32,256,768]{2,1,0:T(8,128)(2,1)} convert(f32[32,256,768]{2,1,0:T(8,128)} %param.4) | non-fusion elementwise | flops 6291456 | bytes 37748736 | tf_op jit(solution)/shard_map/convert_element_type | solution.py:8
  13.8 7.3 %all-to-all-start = ((bf16[32,256,768]{2,1,0:T(8,128)(2,1)}), bf16[32,256,768]{2,1,0:T(8,128)(2,1)}, u32[]{:S(2)}, u32[]{:S(2)}) async-start(bf16[32,256,768]{2,1,0:T(8,128)(2,1)} %convert_element_type.9), calls=%async_computation | async-start | bytes 25165824 | tf_op jit(solution)/shard_map/all_to_all | solution.py:10
  21.1 13.4 %convert_element_type.10 = bf16[32,256,768]{2,1,0:T(8,128)(2,1)} convert(f32[32,256,768]{2,1,0:T(8,128)} %param.5) | non-fusion elementwise | flops 6291456 | bytes 37748736 | tf_op jit(solution)/shard_map/convert_element_type | solution.py:8
  34.5 0.0 copy-start
  34.5 0.0 copy-start.1
  34.5 259.7 %all-to-all-done = bf16[32,256,768]{2,1,0:T(8,128)(2,1)} async-done(((bf16[32,256,768]{2,1,0:T(8,128)(2,1)}), bf16[32,256,768]{2,1,0:T(8,128)(2,1)}, u32[]{:S(2)}, u32[]{:S(2)}) %all-to-all-start) | async-done | bytes 12582944 | tf_op jit(solution)/shard_map/all_to_all | solution.py:10
  294.2 5.3 all-to-all-start.1
  299.5 0.0 copy-done
  299.5 0.0 copy-done.1
  299.5 292.2 %all_gather.6 = bf16[2048,32]{0,1:T(8,128)(2,1)S(1)} all-gather(bf16[256,32]{0,1:T(8,128)(2,1)S(1)} %multiply_convert_fusion), channel_id=1, replica_groups=mesh['owner'=4,'rows'=8] {'rows'}, dimensions={0}, use_global_device_ids=true | all-gather | bytes 147456 | tf_op jit(solution)/shard_map/all_gather | solution.py:16
  591.8 7.2 %all_gather.7 = bf16[2048,128]{0,1:T(8,128)(2,1)S(1)} all-gather(bf16[2048,32]{0,1:T(8,128)(2,1)S(1)} %all_gather.6), channel_id=1, replica_groups=mesh['owner'=4,'rows'=8] {'owner'}, dimensions={1}, use_global_device_ids=true | all-gather | bytes 655360 | tf_op jit(solution)/shard_map/all_gather | solution.py:17
  598.9 1.0 copy.12
  599.9 16.9 %copy.10 = bf16[8,4,256,768]{2,0,3,1:T(8,128)(2,1)} copy(bf16[8,4,256,768]{3,2,1,0:T(8,128)(2,1)} %bitcast) | data formatting | bytes 25165824 | tf_op jit(solution)/shard_map/all_to_all | solution.py:10
  616.8 19.5 %all_to_all.29 = bf16[4,2048,768]{1,2,0:T(8,128)(2,1)} reshape(bf16[4,8,256,768]{2,1,3,0:T(8,128)(2,1)} %bitcast.14) | data formatting | bytes 25165824 | tf_op jit(solution)/shard_map/all_to_all | solution.py:10
  636.3 0.0 all-to-all-done.1
  636.3 16.9 %copy.11 = bf16[8,4,256,768]{2,0,3,1:T(8,128)(2,1)} copy(bf16[8,4,256,768]{3,2,1,0:T(8,128)(2,1)} %bitcast.3) | data formatting | bytes 25165824 | tf_op jit(solution)/shard_map/all_to_all | solution.py:11
  653.2 19.5 %all_to_all.33 = bf16[4,2048,768]{1,2,0:T(8,128)(2,1)} reshape(bf16[4,8,256,768]{2,1,3,0:T(8,128)(2,1)} %bitcast.15) | data formatting | bytes 25165824 | tf_op jit(solution)/shard_map/all_to_all | solution.py:11
  (1 shorter events, 0.0 us)
Async XLA Ops:
  13.8 280.3 %all-to-all-start = ((bf16[32,256,768]{2,1,0:T(8,128)(2,1)}), bf16[32,256,768]{2,1,0:T(8,128)(2,1)}, u32[]{:S(2)}, u32[]{:S(2)}) async-start(bf16[32,256,768]{2,1,0:T(8,128)(2,1)} %convert_element_type.9), calls=%async_computation | async-start | bytes 25165824 | tf_op jit(solution)/shard_map/all_to_all | solution.py:10
  34.5 265.0 %copy-start = (f32[256,32]{0,1:T(8,128)S(1)}, f32[256,32]{0,1:T(8,128)}, u32[]{:S(2)}) copy-start(f32[256,32]{0,1:T(8,128)} %param.6) | copy-start | bytes 98308
  34.5 265.0 %copy-start.1 = (f32[256]{0:T(256)S(1)}, f32[256]{0:T(256)}, u32[]{:S(2)}) copy-start(f32[256]{0:T(256)} %param.7) | copy-start | bytes 3076
  294.2 342.1 %all-to-all-start.1 = ((bf16[32,256,768]{2,1,0:T(8,128)(2,1)}), bf16[32,256,768]{2,1,0:T(8,128)(2,1)}, u32[]{:S(2)}, u32[]{:S(2)}) async-start(bf16[32,256,768]{2,1,0:T(8,128)(2,1)} %convert_element_type.10), calls=%async_computation.1 | async-start | bytes 25165824 | tf_op jit(solution)/shard_map/all_to_all | solution.py:11
where the time goes:
time: 675 us; the launch traced here: 673 us
  blocking collectives  299 us (44%)
  waiting for transfers between devices  260 us (39%)
  local copies, waits for them, and re-layouts  73.7 us (11%)
  other arithmetic  26.6 us (4%)
  starting transfers between devices  12.6 us (2%)
    all_gather x1, blocking collectives, on_device(): row_router = lax.all_gather(part_router, 'rows', axis=0, tiled=True)  292 us
    all_to_all x1, waiting for transfers between devices, on_device(): lax.all_to_all(narrow_gate, 'rows', split_axis=0, concat_axis=1, tiled=True)  260 us
    all_to_all x2, local copies, waits for them, and re-layouts, on_device(): lax.all_to_all(narrow_up, 'rows', split_axis=0, concat_axis=1, tiled=True)  36.4 us
    all_to_all x2, local copies, waits for them, and re-layouts, on_device(): lax.all_to_all(narrow_gate, 'rows', split_axis=0, concat_axis=1, tiled=True)  36.3 us
  transfers between devices with their start and end apart: 2, of which 1 were waited for; matrix products, arithmetic and copies ran while one was open for 5% of the time, Pallas kernels for 0%

commit v1 on v0

--- a/solution.py
+++ b/solution.py
@@ -14,7 +14,7 @@
     ready_up = jnp.transpose(ready_up, (0, 2, 1))
     part_router = (router_weight * router_gain[:, None]).astype(jnp.bfloat16)
     row_router = lax.all_gather(part_router, "rows", axis=0, tiled=True)
-    serve_router = lax.all_gather(row_router, "owner", axis=1, tiled=True)
+    serve_router = jnp.concatenate(lax.all_gather(row_router, "owner"), axis=1)
     return (ready_gate, ready_up, serve_router)
 
 

time: 675 us -> 675 us (level)
  no operation moved by 1% of the time
where the time goes in v1:
time: 675 us; the launch traced here: 673 us
  blocking collectives  299 us (44%)
  waiting for transfers between devices  260 us (39%)
  local copies, waits for them, and re-layouts  74.4 us (11%)
  other arithmetic  26.6 us (4%)
  starting transfers between devices  12.6 us (2%)
    all_gather x1, blocking collectives, on_device(): row_router = lax.all_gather(part_router, 'rows', axis=0, tiled=True)  292 us
    all_to_all x1, waiting for transfers between devices, on_device(): lax.all_to_all(narrow_gate, 'rows', split_axis=0, concat_axis=1, tiled=True)  260 us
    all_to_all x2, local copies, waits for them, and re-layouts, on_device(): lax.all_to_all(narrow_up, 'rows', split_axis=0, concat_axis=1, tiled=True)  36.4 us
    all_to_all x2, local copies, waits for them, and re-layouts, on_device(): lax.all_to_all(narrow_gate, 'rows', split_axis=0, concat_axis=1, tiled=True)  36.3 us
  transfers between devices with their start and end apart: 2, of which 1 were waited for; matrix products, arithmetic and copies ran while one was open for 5% of the time, Pallas kernels for 0%

profile of v1, /device:TPU:0, one launch (start us, length us, event | category | flops | bytes accessed | tf_op | source)
XLA Modules:
  0.0 673.3 jit_solution(9759219024306133304)
XLA Ops:
  0.6 13.2 %convert_element_type.9 = bf16[32,256,768]{2,1,0:T(8,128)(2,1)} convert(f32[32,256,768]{2,1,0:T(8,128)} %param.4) | non-fusion elementwise | flops 6291456 | bytes 37748736 | tf_op jit(solution)/shard_map/convert_element_type | solution.py:8
  13.8 7.3 %all-to-all-start = ((bf16[32,256,768]{2,1,0:T(8,128)(2,1)}), bf16[32,256,768]{2,1,0:T(8,128)(2,1)}, u32[]{:S(2)}, u32[]{:S(2)}) async-start(bf16[32,256,768]{2,1,0:T(8,128)(2,1)} %convert_element_type.9), calls=%async_computation | async-start | bytes 25165824 | tf_op jit(solution)/shard_map/all_to_all | solution.py:10
  21.1 13.4 %convert_element_type.10 = bf16[32,256,768]{2,1,0:T(8,128)(2,1)} convert(f32[32,256,768]{2,1,0:T(8,128)} %param.5) | non-fusion elementwise | flops 6291456 | bytes 37748736 | tf_op jit(solution)/shard_map/convert_element_type | solution.py:8
  34.5 0.0 copy-start
  34.5 0.0 copy-start.1
  34.5 259.7 %all-to-all-done = bf16[32,256,768]{2,1,0:T(8,128)(2,1)} async-done(((bf16[32,256,768]{2,1,0:T(8,128)(2,1)}), bf16[32,256,768]{2,1,0:T(8,128)(2,1)}, u32[]{:S(2)}, u32[]{:S(2)}) %all-to-all-start) | async-done | bytes 12582944 | tf_op jit(solution)/shard_map/all_to_all | solution.py:10
  294.2 5.3 all-to-all-start.1
  299.5 0.0 copy-done
  299.5 0.0 copy-done.1
  299.5 292.2 %all_gather.9 = bf16[2048,32]{0,1:T(8,128)(2,1)S(1)} all-gather(bf16[256,32]{0,1:T(8,128)(2,1)S(1)} %multiply_convert_fusion), channel_id=1, replica_groups=mesh['owner'=4,'rows'=8] {'rows'}, dimensions={0}, use_global_device_ids=true | all-gather | bytes 147456 | tf_op jit(solution)/shard_map/all_gather | solution.py:16
  591.8 7.2 %all-gather = bf16[8192,32]{0,1:T(8,128)(2,1)S(1)} all-gather(bf16[2048,32]{0,1:T(8,128)(2,1)S(1)} %all_gather.9), channel_id=2, replica_groups=mesh['owner'=4,'rows'=8] {'owner'}, dimensions={0}, use_global_device_ids=true | all-gather | bytes 655360 | tf_op jit(solution)/shard_map/all_gather | solution.py:17
  598.9 0.4 reshape.15
  599.3 0.3 copy.15
  599.6 1.0 copy.16
  600.6 16.9 %copy.13 = bf16[8,4,256,768]{2,0,3,1:T(8,128)(2,1)} copy(bf16[8,4,256,768]{3,2,1,0:T(8,128)(2,1)} %bitcast) | data formatting | bytes 25165824 | tf_op jit(solution)/shard_map/all_to_all | solution.py:10
  617.5 19.5 %all_to_all.29 = bf16[4,2048,768]{1,2,0:T(8,128)(2,1)} reshape(bf16[4,8,256,768]{2,1,3,0:T(8,128)(2,1)} %bitcast.18) | data formatting | bytes 25165824 | tf_op jit(solution)/shard_map/all_to_all | solution.py:10
  637.0 0.0 all-to-all-done.1
  637.0 16.9 %copy.14 = bf16[8,4,256,768]{2,0,3,1:T(8,128)(2,1)} copy(bf16[8,4,256,768]{3,2,1,0:T(8,128)(2,1)} %bitcast.3) | data formatting | bytes 25165824 | tf_op jit(solution)/shard_map/all_to_all | solution.py:11
  653.9 19.5 %all_to_all.33 = bf16[4,2048,768]{1,2,0:T(8,128)(2,1)} reshape(bf16[4,8,256,768]{2,1,3,0:T(8,128)(2,1)} %bitcast.19) | data formatting | bytes 25165824 | tf_op jit(solution)/shard_map/all_to_all | solution.py:11
  (1 shorter events, 0.0 us)
Async XLA Ops:
  13.8 280.3 %all-to-all-start = ((bf16[32,256,768]{2,1,0:T(8,128)(2,1)}), bf16[32,256,768]{2,1,0:T(8,128)(2,1)}, u32[]{:S(2)}, u32[]{:S(2)}) async-start(bf16[32,256,768]{2,1,0:T(8,128)(2,1)} %convert_element_type.9), calls=%async_computation | async-start | bytes 25165824 | tf_op jit(solution)/shard_map/all_to_all | solution.py:10
  34.5 265.0 %copy-start = (f32[256,32]{0,1:T(8,128)S(1)}, f32[256,32]{0,1:T(8,128)}, u32[]{:S(2)}) copy-start(f32[256,32]{0,1:T(8,128)} %param.6) | copy-start | bytes 98308
  34.5 265.0 %copy-start.1 = (f32[256]{0:T(256)S(1)}, f32[256]{0:T(256)}, u32[]{:S(2)}) copy-start(f32[256]{0:T(256)} %param.7) | copy-start | bytes 3076
  294.2 342.8 %all-to-all-start.1 = ((bf16[32,256,768]{2,1,0:T(8,128)(2,1)}), bf16[32,256,768]{2,1,0:T(8,128)(2,1)}, u32[]{:S(2)}, u32[]{:S(2)}) async-start(bf16[32,256,768]{2,1,0:T(8,128)(2,1)} %convert_element_type.10), calls=%async_computation.1 | async-start | bytes 25165824 | tf_op jit(solution)/shard_map/all_to_all | solution.py:11
